TPU v7x, 32 devices: a whole 2x2x4 slice. The times are simulated.
32 devices in a mesh: cells: 16 (over z, y, core), genes: 2 (over x).
Axes of the slice: x: 2, y: 2, z: 4, core: 2. Of those that a mesh axis runs over, the one named last changes fastest.
Arguments:
- counts: int32 [2048, 33280], P('cells', 'genes'), may hold values from 0 to 64, as said below
- live_rows: int32 [16], P('cells'), may hold values from 64 to 128, as said below
- left_basis: float32 [32, 2048], P(None, 'cells'), may hold values from -0.125 to 0.125
- right_basis: float32 [32, 33280], P(None, 'genes'), may hold values from -0.03125 to 0.03125
- right_start: float32 [16, 33280], P(None, 'genes'), may hold values from -0.03125 to 0.03125
Outputs:
- left_vectors: float32 [48, 2048], P(None, 'cells')
- right_vectors: float32 [48, 33280], P(None, 'genes')
- diag_blocks: float32 [3, 16, 16], replicated
- couple_blocks: float32 [3, 16, 16], replicated
Inputs may be any that keep to these rules, and one draw needn't show every extreme that they name: `counts`: rows of a cell block at or beyond its live count are padding and are not part of the matrix. `live_rows`: entry b is the number of live rows, the first ones, of cell block b; some block is full in every draw.
All inputs are finite; a program needn't handle non-finite values.
Results may differ from a plain program's by a relative error of at most 0.0003.
Values sent between devices are 32-bit elements; how exact they have to be, the bound alone decides.
A program may use at most 64 MiB of HBM per device.

v0:
```python
import math

import jax
import jax.numpy as jnp
from jax import lax
from jax.sharding import PartitionSpec as P

BASIS = 32
BLOCK = 16
STEPS = 3


HIGHEST = lax.Precision.HIGHEST


def matmul(lhs, rhs):
    return jnp.dot(lhs, rhs, precision=HIGHEST, preferred_element_type=jnp.float32)


def outer_rows(lhs, rhs):
    return lax.dot_general(
        lhs, rhs, (((1,), (1,)), ((), ())), precision=HIGHEST, preferred_element_type=jnp.float32
    )


def lower_solve(factor, values):
    return lax.linalg.triangular_solve(factor, values, left_side=True, lower=True)


def orthonormal_block(vectors, spanning, correlations, position, totals, stored):
    width = vectors.shape[0]
    coeffs, squares = totals((outer_rows(vectors, spanning), outer_rows(vectors, vectors)))
    combined = coeffs + coeffs - matmul(coeffs, correlations)
    cleaned = vectors - matmul(combined, spanning)
    crossed = outer_rows(combined, coeffs)
    squares = squares - crossed - crossed.T + outer_rows(matmul(combined, correlations), combined)
    factor = jnp.linalg.cholesky(squares)
    result = lower_solve(factor, cleaned)
    if stored:
        against = lower_solve(factor, coeffs - matmul(combined, correlations))
        self_term = lower_solve(factor, lower_solve(factor, squares).T)
        correlations = correlations.at[position : position + width, :].set(against)
        correlations = correlations.at[:, position : position + width].set(against.T)
        correlations = correlations.at[
            position : position + width, position : position + width
        ].set(self_term)
    if stored:
        spanning = spanning.at[position : position + width].set(result)
    return (result, factor, spanning, correlations)


def body(counts, live_rows, left_basis, right_basis, right_start):
    cell_rows, gene_cols = counts.shape
    live_here = live_rows[0]
    weights = (jnp.arange(cell_rows, dtype=jnp.int32) < live_here).astype(jnp.float32)
    logged = jnp.where(weights[:, None] > 0, jnp.log1p(counts.astype(jnp.float32)), 0.0)
    column_total, live_total = lax.psum(
        (jnp.sum(logged, axis=0), live_here.astype(jnp.float32)), "cells"
    )
    column_mean = column_total / live_total
    factor_scale = lax.rsqrt(live_total)
    slots_left = jnp.concatenate(
        [left_basis * weights[None, :], jnp.zeros((STEPS * BLOCK, cell_rows), jnp.float32)], axis=0
    )
    slots_right = jnp.concatenate(
        [right_basis, right_start, jnp.zeros(((STEPS - 1) * BLOCK, gene_cols), jnp.float32)], axis=0
    )

    def left_totals(values):
        return lax.psum(values, "cells")

    def right_totals(values):
        return lax.psum(values, "genes")

    correlation_left = left_totals(outer_rows(slots_left, slots_left))
    correlation_right = right_totals(outer_rows(slots_right, slots_right))
    current = right_start
    left_blocks, right_blocks, diag_list, couple_list = ([], [], [], [])
    for iteration in range(STEPS):
        position = BASIS + iteration * BLOCK
        projected = (
            outer_rows(current, logged) - matmul(current, column_mean)[:, None] * weights[None, :]
        ) * factor_scale
        leftvec, diag_factor, slots_left, correlation_left = orthonormal_block(
            lax.psum(projected, "genes"), slots_left, correlation_left, position, left_totals, True
        )
        projected = (
            matmul(leftvec, logged) - jnp.sum(leftvec, axis=1)[:, None] * column_mean[None, :]
        ) * factor_scale
        rightvec, side_factor, slots_right, correlation_right = orthonormal_block(
            lax.psum(projected, "cells"),
            slots_right,
            correlation_right,
            position + BLOCK,
            right_totals,
            iteration + 1 < STEPS,
        )
        current = rightvec
        left_blocks.append(leftvec)
        right_blocks.append(current)
        diag_list.append(diag_factor)
        couple_list.append(side_factor)
    cells_total = cell_rows * lax.axis_size("cells")
    genes_total = gene_cols * lax.axis_size("genes")
    left_vectors = jnp.concatenate(left_blocks, axis=0) * math.sqrt(float(cells_total))
    right_vectors = jnp.concatenate(right_blocks, axis=0) * math.sqrt(float(genes_total))
    return (left_vectors, right_vectors, jnp.stack(diag_list), jnp.stack(couple_list))


def solution(mesh):
    in_specs = (
        P("cells", "genes"),
        P("cells"),
        P(None, "cells"),
        P(None, "genes"),
        P(None, "genes"),
    )
    out_specs = (P(None, "cells"), P(None, "genes"), P(), P())
    return jax.shard_map(body, mesh=mesh, in_specs=in_specs, out_specs=out_specs, check_vma=False)
```

profile of v0, /device:TPU:0, one launch (start us, length us, event | category | flops | bytes accessed | tf_op | source)
XLA Modules:
  0.0 750.8 jit_solution(15386551150408046727)
XLA Ops:
  7.9 7.7 %fusion.66 = f32[16640]{0:T(1024)} fusion(s32[128,16640]{1,0:T(8,128)} %param.46, pred[128]{0:T(512)(128)(4,1)S(1)} %broadcast_compare_fusion), kind=kLoop, calls=%fused_computation.158 | loop fusion | flops 6373120 | bytes 8586368 | tf_op jit(solution)/shard_map/reduce_sum | solution.py:58
  23.0 35.7 %psum.155 = f32[]{:T(128)} all-reduce(f32[]{:T(128)S(6)} %convert_element_type.19), channel_id=1, replica_groups=mesh['cells'=16,'genes'=2] {'cells'}, use_global_device_ids=true, to_apply=%region_2.3 | all-reduce | flops 1 | bytes 8 | tf_op jit(solution)/shard_map/psum | solution.py:57
  60.7 44.6 %all-reduce.12.cloned.1.call-done = f32[16640]{0:T(1024)} async-done(((f32[16640]{0:T(1024)}), f32[16640]{0:T(1024)}) %all-reduce.12.cloned.1.call-update) | async-done | bytes 66576 | tf_op jit(solution)/shard_map/psum | solution.py:57
  108.2 12.2 %fusion.6 = f32[16,128]{1,0:T(8,128)S(1)} fusion(f32[16,16640]{1,0:T(8,128)S(1)} %copy-done, f32[]{:T(128)S(6)} %rsqrt.3, f32[128]{0:T(128)S(1)} %compare_convert_fusion, f32[16]{0:T(128)S(1)} %convolution_bitcast_fusion.7, s32[128,16640]{1,0:T(8,128)} %param.46, pred[128]{0:T(512)(128)(4,1)S(1)} %broadcast_compare_fusion), kind=kOutput, calls=%fused_computation.37 | convolution fusion | flops 413210624 | bytes 9593540 | tf_op jit(solution)/shard_map/dot_general | solution.py:21
  120.4 5.0 psum.156
  125.6 58.8 %all-reduce.3 = (f32[16,80]{1,0:T(8,128)S(1)}, f32[80,80]{1,0:T(8,128)S(1)}, f32[16,16]{0,1:T(8,128)S(1)}) all-reduce(f32[16,80]{1,0:T(8,128)S(1)} %fusion.10, f32[80,80]{1,0:T(8,128)S(1)} %fusion.8, f32[16,16]{0,1:T(8,128)S(1)} %fusion.68), channel_id=1, replica_groups=mesh['cells'=16,'genes'=2] {'cells'}, use_global_device_ids=true, to_apply=%region_5.6 | all-reduce | flops 7936 | bytes 63488 | tf_op jit(solution)/shard_map/psum | solution.py:70
  189.8 10.2 %fusion.2 = f32[16,16640]{1,0:T(8,128)} fusion(f32[16,128]{1,0:T(8,128)S(1)} %get-tuple-element.231, f32[]{:T(128)S(6)} %rsqrt.3, f32[16640]{0:T(1024)S(1)} %broadcast_divide_fusion, f32[16]{0:T(128)S(1)} %get-tuple-element.230, s32[128,16640]{1,0:T(8,128)} %param.46, pred[128]{0:T(512)(128)(4,1)S(1)} %broadcast_compare_fusion), kind=kOutput, calls=%fused_computation.8 | convolution fusion | flops 414003200 | bytes 9659588 | tf_op jit(solution)/shard_map/dot_general | solution.py:17
  202.9 88.5 %all-reduce.14.cloned.1.call-done = f32[16,16640]{1,0:T(8,128)} async-done(((f32[16,16640]{1,0:T(8,128)}), f32[16,16640]{1,0:T(8,128)}) %all-reduce.14.cloned.1.call-update) | async-done | bytes 1064976 | tf_op jit(solution)/shard_map/psum | solution.py:91
  291.4 6.3 fusion.65
  299.2 8.7 %all-reduce.6 = (f32[16,80]{1,0:T(8,128)S(1)}, f32[80,80]{1,0:T(8,128)S(1)}, f32[16,16]{0,1:T(8,128)S(1)}) all-reduce(f32[16,80]{1,0:T(8,128)S(1)} %fusion.65, f32[80,80]{1,0:T(8,128)S(1)} %fusion.64, f32[16,16]{0,1:T(8,128)S(1)} %fusion.71), channel_id=1, replica_groups=mesh['cells'=16,'genes'=2] {'genes'}, use_global_device_ids=true, to_apply=%region_12.0 | all-reduce | flops 7936 | bytes 63488 | tf_op jit(solution)/shard_map/psum | solution.py:73
  320.3 11.9 %fusion.4 = f32[16,128]{1,0:T(8,128)S(1)} fusion(f32[16,16640]{1,0:T(8,128)S(1)} %get-tuple-element.236, f32[16]{0:T(128)S(1)} %convolution_bitcast_fusion.6, f32[]{:T(128)S(6)} %rsqrt.3, f32[128]{0:T(128)S(1)} %compare_convert_fusion, s32[128,16640]{1,0:T(8,128)} %param.46, pred[128]{0:T(512)(128)(4,1)S(1)} %broadcast_compare_fusion), kind=kOutput, calls=%fused_computation.29 | convolution fusion | flops 413210624 | bytes 9593540 | tf_op jit(solution)/shard_map/dot_general | solution.py:21
  332.2 5.0 psum.164
  337.5 57.9 %all-reduce.2 = (f32[16,80]{1,0:T(8,128)S(1)}, f32[16,16]{0,1:T(8,128)S(1)}) all-reduce(f32[16,80]{1,0:T(8,128)S(1)} %fusion.75, f32[16,16]{0,1:T(8,128)S(1)} %fusion.74), channel_id=1, replica_groups=mesh['cells'=16,'genes'=2] {'cells'}, use_global_device_ids=true, to_apply=%region_16.20 | all-reduce | flops 1536 | bytes 12288 | tf_op jit(solution)/shard_map/psum | solution.py:70
  401.2 10.2 %fusion.1 = f32[16,16640]{1,0:T(8,128)} fusion(f32[16,128]{1,0:T(8,128)S(1)} %get-tuple-element.234, f32[16]{0:T(128)S(1)} %get-tuple-element.228, f32[]{:T(128)S(6)} %rsqrt.3, f32[16640]{0:T(1024)S(1)} %broadcast_divide_fusion, s32[128,16640]{1,0:T(8,128)} %param.46, pred[128]{0:T(512)(128)(4,1)S(1)} %broadcast_compare_fusion), kind=kOutput, calls=%fused_computation.5 | convolution fusion | flops 414003200 | bytes 9659588 | tf_op jit(solution)/shard_map/dot_general | solution.py:17
  415.3 86.6 %all-reduce.16.cloned.1.call-done = f32[16,16640]{1,0:T(8,128)} async-done(((f32[16,16640]{1,0:T(8,128)}), f32[16,16640]{1,0:T(8,128)}) %all-reduce.16.cloned.1.call-update) | async-done | bytes 1064976 | tf_op jit(solution)/shard_map/psum | solution.py:91
  505.0 6.2 fusion.79
  511.2 8.2 %all-reduce.5 = (f32[16,80]{1,0:T(8,128)S(1)}, f32[16,16]{0,1:T(8,128)S(1)}) all-reduce(f32[16,80]{1,0:T(8,128)S(1)} %fusion.79, f32[16,16]{0,1:T(8,128)S(1)} %fusion.78), channel_id=1, replica_groups=mesh['cells'=16,'genes'=2] {'genes'}, use_global_device_ids=true, to_apply=%region_21.27 | all-reduce | flops 1536 | bytes 12288 | tf_op jit(solution)/shard_map/psum | solution.py:73
  532.4 11.9 %fusion.3 = f32[16,128]{1,0:T(8,128)S(1)} fusion(f32[16,16640]{1,0:T(8,128)S(1)} %get-tuple-element.244, f32[16]{0:T(128)S(1)} %convolution_bitcast_fusion.5, f32[]{:T(128)S(6)} %rsqrt.3, f32[128]{0:T(128)S(1)} %compare_convert_fusion, s32[128,16640]{1,0:T(8,128)} %param.46, pred[128]{0:T(512)(128)(4,1)S(1)} %broadcast_compare_fusion), kind=kOutput, calls=%fused_computation.20 | convolution fusion | flops 413210624 | bytes 9593540 | tf_op jit(solution)/shard_map/dot_general | solution.py:21
  544.3 5.0 psum.170
  549.5 58.0 %all-reduce.1 = (f32[16,80]{1,0:T(8,128)S(1)}, f32[16,16]{0,1:T(8,128)S(1)}) all-reduce(f32[16,80]{1,0:T(8,128)S(1)} %fusion.83, f32[16,16]{0,1:T(8,128)S(1)} %fusion.82), channel_id=1, replica_groups=mesh['cells'=16,'genes'=2] {'cells'}, use_global_device_ids=true, to_apply=%region_25.31 | all-reduce | flops 1536 | bytes 12288 | tf_op jit(solution)/shard_map/psum | solution.py:70
  612.8 10.2 %fusion = f32[16,16640]{1,0:T(8,128)} fusion(f32[16,128]{1,0:T(8,128)S(1)} %get-tuple-element.242, f32[16]{0:T(128)S(1)} %get-tuple-element.241, f32[]{:T(128)S(6)} %rsqrt.3, f32[16640]{0:T(1024)S(1)} %broadcast_divide_fusion, s32[128,16640]{1,0:T(8,128)} %param.46, pred[128]{0:T(512)(128)(4,1)S(1)} %broadcast_compare_fusion), kind=kOutput, calls=%fused_computation.2 | convolution fusion | flops 414003200 | bytes 9659588 | tf_op jit(solution)/shard_map/dot_general | solution.py:17
  625.9 87.7 %all-reduce.18.cloned.1.call-done = f32[16,16640]{1,0:T(8,128)} async-done(((f32[16,16640]{1,0:T(8,128)}), f32[16,16640]{1,0:T(8,128)}) %all-reduce.18.cloned.1.call-update) | async-done | bytes 1064976 | tf_op jit(solution)/shard_map/psum | solution.py:91
  716.7 6.2 fusion.87
  722.9 8.0 %all-reduce.4 = (f32[16,80]{1,0:T(8,128)S(1)}, f32[16,16]{0,1:T(8,128)S(1)}) all-reduce(f32[16,80]{1,0:T(8,128)S(1)} %fusion.87, f32[16,16]{0,1:T(8,128)S(1)} %fusion.86), channel_id=1, replica_groups=mesh['cells'=16,'genes'=2] {'genes'}, use_global_device_ids=true, to_apply=%region_29.35 | all-reduce | flops 1536 | bytes 12288 | tf_op jit(solution)/shard_map/psum | solution.py:73
  (159 shorter events, 84.4 us)
Async XLA Ops:
  7.2 98.1 %all-reduce.12.cloned.1.call-start = ((), (), s32[]{:S(2)}) async-start(), calls=%async_computation | async-start | bytes 139264 | tf_op jit(solution)/shard_map/psum | solution.py:57
  7.9 7.9 %copy-start = (f32[16,16640]{1,0:T(8,128)S(1)}, f32[16,16640]{1,0:T(8,128)}, u32[]{:S(2)}) copy-start(f32[16,16640]{1,0:T(8,128)} %param.50) | copy-start | bytes 3194884
  7.9 7.9 %copy-start.4 = (f32[32,16640]{1,0:T(8,128)S(1)}, f32[32,16640]{1,0:T(8,128)}, u32[]{:S(2)}) copy-start(f32[32,16640]{1,0:T(8,128)} %param.49) | copy-start | bytes 6389764
  15.6 275.8 %all-reduce.14.cloned.1.call-start = ((), (), s32[]{:S(2)}) async-start(), calls=%async_computation.1 | async-start | bytes 2129920 | tf_op jit(solution)/shard_map/psum | solution.py:91
  20.1 2.8 copy-start.5
  200.0 301.8 %all-reduce.16.cloned.1.call-start = ((), (), s32[]{:S(2)}) async-start(), calls=%async_computation.2 | async-start | bytes 2129920 | tf_op jit(solution)/shard_map/psum | solution.py:91
  291.4 6.3 copy-start.3
  411.4 302.2 %all-reduce.18.cloned.1.call-start = ((), (), s32[]{:S(2)}) async-start(), calls=%async_computation.3 | async-start | bytes 2129920 | tf_op jit(solution)/shard_map/psum | solution.py:91
  501.8 3.2 copy-start.1
  713.5 3.2 copy-start.2
Sparse Core Ops, SparseCore 0:
  15.7 89.5 all-reduce.11
  200.2 91.1 all-reduce.13
  411.5 90.2 all-reduce.15
  623.1 90.3 all-reduce.17
where the time goes:
time: 758 us; the launch traced here: 751 us
  waiting for transfers between devices  307 us (41%)
  blocking collectives  250 us (33%)
  matrix products  128 us (17%)
  other arithmetic  42.6 us (6%)
  between operations  15.9 us (2%)
    psum x3, waiting for transfers between devices, body(): lax.psum(projected, 'cells')  263 us
    psum x3, blocking collectives, left_totals(): return lax.psum(values, 'cells')  175 us
    dot_general x29, matrix products, outer_rows(): lax.dot_general(lhs, rhs, (((1,), (1,)), ((), ())), precision=HIGHEST, pr...  69.6 us
    dot_general x24, matrix products, matmul(): jnp.dot(lhs, rhs, precision=HIGHEST, preferred_element_type=jnp.float32)  49.9 us
    psum x1, waiting for transfers between devices, body(): lax.psum((jnp.sum(logged, axis=0), live_here.astype(jnp.float32)), 'cells')  44.6 us
    psum x1, blocking collectives, body(): lax.psum((jnp.sum(logged, axis=0), live_here.astype(jnp.float32)), 'cells')  35.7 us
    psum x3, blocking collectives, right_totals(): return lax.psum(values, 'genes')  24.9 us
  transfers between devices with their start and end apart: 4, of which 4 were waited for; matrix products, arithmetic and copies ran while one was open for 2% of the time, Pallas kernels for 0%

commit v1 on v0

v1 whole, which is shorter than its diff:
```python
import functools
import math

import jax
import jax.numpy as jnp
from jax import lax
from jax.experimental import pallas as pl
from jax.experimental.pallas import tpu as pltpu
from jax.sharding import PartitionSpec as P

BASIS = 32
BLOCK = 16
STEPS = 3
SLOTS = BASIS + STEPS * BLOCK
LANES = 128
F32 = jnp.float32
BF16 = jnp.bfloat16
HIGHEST = lax.Precision.HIGHEST
MESH = pl.DeviceIdType.MESH


def exact(lhs, rhs):
    return jnp.dot(lhs, rhs, precision=HIGHEST, preferred_element_type=F32)


def exact_rows(lhs, rhs):
    return lax.dot_general(
        lhs, rhs, (((1,), (1,)), ((), ())), precision=HIGHEST, preferred_element_type=F32
    )


def split(values):
    high = values.astype(BF16)
    return high, (values - high.astype(F32)).astype(BF16)


def product(high, both, rhs_high, rhs_low, dims):
    rows = high.shape[0]
    first = lax.dot_general(both, rhs_high, (dims, ((), ())), preferred_element_type=F32)
    second = lax.dot_general(high, rhs_low, (dims, ((), ())), preferred_element_type=F32)
    return first[:rows] + (first[rows:] + second)


ALONG = ((1,), (0,))
ROWS = ((1,), (1,))


def loop(start, stop, step):
    def one(k, carry):
        step(k)
        return carry

    lax.fori_loop(start, stop, one, 0)


def orthonormal(gram, near, lower, spanning, vectors):
    lane = lax.broadcasted_iota(jnp.int32, (BLOCK, LANES), 1)
    row = lax.broadcasted_iota(jnp.int32, (BLOCK, LANES), 0)
    coeffs = jnp.where(lane < SLOTS, gram, 0.0)
    squares = gram[:, SLOTS : SLOTS + BLOCK]
    combined = coeffs + coeffs - (exact(coeffs, near) + exact_rows(coeffs, lower))
    residue = coeffs - (exact(combined, near) + exact_rows(combined, lower))
    squares = squares - exact_rows(combined, coeffs) - exact_rows(residue, combined)
    cleaned = vectors - exact(combined, spanning)
    change = jnp.where(lane == row + SLOTS, 1.0, -combined)
    parts = [squares, cleaned, residue, change]
    for k in range(BLOCK):
        pivot = parts[0][k : k + 1, k : k + 1]
        root = lax.rsqrt(pivot)
        root = root * (1.5 - 0.5 * pivot * root * root)
        column = parts[0][:, k : k + 1] * root
        after = []
        for part in parts:
            scaled = part[k : k + 1, :] * root
            places = lax.broadcasted_iota(jnp.int32, part.shape, 0)
            after.append(
                jnp.where(places > k, part - column * scaled, jnp.where(places == k, scaled, part))
            )
        parts = after
    spot = lax.broadcasted_iota(jnp.int32, (BLOCK, BLOCK), 0)
    other = lax.broadcasted_iota(jnp.int32, (BLOCK, BLOCK), 1)
    upper = jnp.where(other >= spot, parts[0], 0.0)
    factor = exact_rows(jnp.where(other == spot, 1.0, 0.0).astype(F32), upper)
    return parts[1], factor, parts[2], parts[3]


def kernel(
    n, g, width, scales,
    live, counts, left_basis, right_basis, right_start,
    left_out, right_out, diag_out, couple_out,
    cnt, logged, bhi, blo, rb, sl, mr, el, tl, er, tr,
    w, ra, rt, pb, w8, ra8, rt8, pb8, gram0, gram, xg0, xg,
    in_sem, as_sem, ar_sem, bs_sem, br_sem, cs_sem, cr_sem, ds_sem,
    g0s_sem, g0r_sem, gs_sem, gr_sem, x0s_sem, x0r_sem, xs_sem, xr_sem,
):
    cells, genes = counts.shape
    me = lax.axis_index("cells")
    mine = lax.axis_index("genes")
    core = lax.rem(me, 2)
    chip = me // 2
    h = n // 2
    sibling = me + 1 - 2 * core

    def along_cells(src, dst, send, recv, peer):
        return pltpu.make_async_remote_copy(
            src_ref=src, dst_ref=dst, send_sem=send, recv_sem=recv,
            device_id=(peer, mine), device_id_type=MESH,
        )

    def along_genes(src, dst, send, recv, peer):
        return pltpu.make_async_remote_copy(
            src_ref=src, dst_ref=dst, send_sem=send, recv_sem=recv,
            device_id=(me, peer), device_id_type=MESH,
        )

    loads = []
    for d in range(n):
        cols = max(0, min(width, genes - d * width))
        if cols:
            here = pl.ds(d * width, cols)
            loads.append((d, [
                pltpu.make_async_copy(counts.at[:, here], cnt.at[d, :, pl.ds(0, cols)], in_sem.at[d, 0]),
                pltpu.make_async_copy(right_basis.at[:, here], rb.at[d, pl.ds(0, BASIS), pl.ds(0, cols)], in_sem.at[d, 1]),
                pltpu.make_async_copy(right_start.at[:, here], rb.at[d, pl.ds(BASIS, BLOCK), pl.ds(0, cols)], in_sem.at[d, 2]),
            ]))
        if cols < width:
            cnt[d, :, cols:] = jnp.zeros((cells, width - cols), jnp.int32)
            rb[d, :, cols:] = jnp.zeros((BASIS + BLOCK, width - cols), F32)
    for _, trio in loads:
        trio[0].start()
    for _, trio in loads:
        trio[1].start()
        trio[2].start()

    barrier = pltpu.get_barrier_semaphore()

    def greet_cells(k):
        pl.semaphore_signal(barrier, inc=1, device_id=(lax.rem(me + k, n), mine), device_id_type=MESH)

    def greet_genes(k):
        pl.semaphore_signal(barrier, inc=1, device_id=(me, lax.rem(mine + k, g)), device_id_type=MESH)

    loop(1, n, greet_cells)
    loop(1, g, greet_genes)
    pl.semaphore_wait(barrier, n - 1 + g - 1)

    def spread(copy, buf, at, size, send, recv):
        def go(k):
            copy(buf.at[at], buf.at[at], send.at[k], recv.at[at], lax.rem(at + k, size)).start()

        loop(1, size, go)

    def gathered(copy, buf, at, size, send, recv):
        def end(k):
            source = lax.rem(at + size - k, size)
            item = copy(buf.at[source], buf.at[source], send.at[k], recv.at[source], lax.rem(at + k, size))
            item.wait_send()
            item.wait_recv()

        loop(1, size, end)
        return lax.fori_loop(
            1, size, lambda k, total: total + buf[k], buf[0]
        )

    def reduce_scatter(produce, part, fromcore, fromchips, result):
        def first(k):
            t = lax.rem(chip + 1 + k, h)
            d = 2 * t + 1 - core
            produce(d)
            along_cells(part.at[d], fromcore.at[t], as_sem.at[t], ar_sem.at[t], sibling).start()

        loop(0, h, first)

        def join(t):
            d = 2 * t + core
            produce(d)
            along_cells(part.at[d], fromcore.at[t], as_sem.at[t], ar_sem.at[t], sibling).wait_recv()
            part[d] = part[d] + fromcore[t]
            return d

        def second(k):
            t = lax.rem(chip + 1 + k, h)
            d = join(t)
            along_cells(part.at[d], fromchips.at[chip], bs_sem.at[t], br_sem.at[chip], d).start()

        loop(0, h - 1, second)
        join(chip)
        result[me] = part[me]

        def third(k):
            t = lax.rem(chip + h - k, h)
            along_cells(part.at[me], fromchips.at[t], bs_sem.at[t], br_sem.at[t], sibling).wait_recv()
            result[me] = result[me] + fromchips[t]

        loop(1, h, third)

    def all_gather(part, fromcore, fromchips, result, consume):
        def go(k):
            t = lax.rem(chip + k, h)
            along_cells(result.at[me], result.at[me], cs_sem.at[t], cr_sem.at[me], 2 * t + core).start()

        loop(1, h, go)
        along_cells(result.at[me], result.at[me], ds_sem.at[chip], cr_sem.at[me], sibling).start()
        consume(me)

        def pass_on(k):
            t = lax.rem(chip + h - k, h)
            d = 2 * t + core
            along_cells(result.at[d], result.at[d], cs_sem.at[t], cr_sem.at[d], sibling).wait_recv()
            along_cells(result.at[d], result.at[d], ds_sem.at[t], cr_sem.at[d], sibling).start()
            consume(d)

        loop(1, h, pass_on)

        def rest(k):
            t = lax.rem(chip + h - k, h)
            d = 2 * t + 1 - core
            along_cells(result.at[d], result.at[d], cs_sem.at[t], cr_sem.at[d], sibling).wait_recv()
            consume(d)

        loop(0, h, rest)

        def ended(t):
            along_cells(part.at[t], fromcore.at[t], as_sem.at[t], ar_sem.at[t], sibling).wait_send()
            along_cells(result.at[t], result.at[t], ds_sem.at[t], cr_sem.at[t], sibling).wait_send()

        loop(0, h, ended)

        def ended_chips(k):
            t = lax.rem(chip + k, h)
            along_cells(part.at[t], fromchips.at[t], bs_sem.at[t], br_sem.at[t], sibling).wait_send()
            along_cells(result.at[t], result.at[t], cs_sem.at[t], cr_sem.at[t], sibling).wait_send()

        loop(1, h, ended_chips)

    live_here = live[0]
    weights_row = jnp.where(
        lax.broadcasted_iota(jnp.int32, (1, cells), 1) < live_here, 1.0, 0.0
    ).astype(F32)
    weights = jnp.where(
        lax.broadcasted_iota(jnp.int32, (cells, LANES), 0) < live_here, 1.0, 0.0
    ).astype(F32)
    for table in (sl, mr, tl, tr):
        table[...] = jnp.zeros_like(table)
    same = jnp.where(
        lax.broadcasted_iota(jnp.int32, (LANES, LANES), 0)
        == lax.broadcasted_iota(jnp.int32, (LANES, LANES), 1),
        1.0, 0.0,
    ).astype(F32)
    el[...] = same
    er[...] = same
    sl[0:BASIS] = left_basis[...] * weights_row
    gram0[me] = exact_rows(sl[0:BASIS], sl[...])
    spread(along_cells, gram0, me, n, g0s_sem, g0r_sem)

    for _, trio in loads:
        trio[0].wait()
    tiles = width // LANES

    def take_log(d):
        for i in range(tiles):
            here = slice(i * LANES, (i + 1) * LANES)
            values = jnp.log(1.0 + cnt[d, :, here].astype(F32)) * weights
            logged[d, :, here] = values
            w8[d, :, here] = jnp.sum(values.reshape(cells // 8, 8, LANES), axis=0)

    loop(0, n, take_log)
    total_at, total_lane = genes // width, genes % width
    w8[total_at, :, total_lane : total_lane + LANES] = jnp.where(
        lax.broadcasted_iota(jnp.int32, (8, LANES), 0) == 0, live_here.astype(F32), 0.0
    )

    reduce_scatter(lambda d: None, w8, ra8, rt8, pb8)
    for _, trio in loads:
        trio[1].wait()
        trio[2].wait()

    def fill(d):
        high, low = split(rb[d])
        bhi[d, cells : cells + BASIS + BLOCK] = high
        blo[d, cells : cells + BASIS + BLOCK] = low
        blank = jnp.zeros((LANES - BASIS - BLOCK, width), BF16)
        bhi[d, cells + BASIS + BLOCK :] = blank
        blo[d, cells + BASIS + BLOCK :] = blank

    loop(0, n, fill)
    all_gather(w8, ra8, rt8, pb8, lambda d: None)
    live_total = jnp.sum(
        pb8[total_at, :, total_lane : total_lane + LANES], axis=0, keepdims=True
    )
    inverse = 1.0 / live_total
    factor_scale = lax.rsqrt(live_total)
    factor_scale = factor_scale * (1.5 - 0.5 * live_total * factor_scale * factor_scale)

    xg0[mine] = jnp.zeros((BASIS + BLOCK, 2 * LANES), F32)

    def center(d):
        for i in range(tiles):
            here = slice(i * LANES, (i + 1) * LANES)
            mean = jnp.sum(pb8[d, :, here], axis=0, keepdims=True) * inverse
            mean = jnp.where(d * width + i * LANES < genes, mean, 0.0)
            high, low = split((logged[d, :, here] - weights * mean) * factor_scale)
            bhi[d, 0:cells, here] = high
            blo[d, 0:cells, here] = low
        high, low = split(rb[d])
        both = jnp.concatenate([high, low], axis=0)
        xg0[mine] = xg0[mine] + product(high, both, bhi[d], blo[d], ROWS)

    loop(0, n, center)
    spread(along_genes, xg0, mine, g, x0s_sem, x0r_sem)
    el[0:BASIS] = gathered(along_cells, gram0, me, n, g0s_sem, g0r_sem)
    el[...] = jnp.where((same > 0) & (lax.broadcasted_iota(jnp.int32, (LANES, LANES), 0) >= BASIS), 1.0, el[...])
    cross = gathered(along_genes, xg0, mine, g, x0s_sem, x0r_sem)
    mr[0 : BASIS + BLOCK] = cross[:, :cells]
    er[0 : BASIS + BLOCK] = cross[:, cells:]
    whole = genes // width

    def step(j):
        position = pl.multiple_of(BASIS + j * BLOCK, BLOCK)
        vectors = mr[pl.ds(position, BLOCK)]
        sl[SLOTS : SLOTS + BLOCK] = vectors
        gram[me] = exact_rows(vectors, sl[...])
        spread(along_cells, gram, me, n, gs_sem, gr_sem)
        total = gathered(along_cells, gram, me, n, gs_sem, gr_sem)
        leftvec, factor, against, _ = orthonormal(total, el[...], tl[...], sl[...], vectors)
        diag_out[j] = factor
        sl[pl.ds(position, BLOCK)] = leftvec
        el[pl.ds(position, BLOCK)] = el[pl.ds(position, BLOCK)] + against
        tl[pl.ds(position, BLOCK)] = against
        left_out[pl.ds(position - BASIS, BLOCK)] = leftvec * scales[0]
        high, low = split(leftvec)
        both = jnp.concatenate([high, low], axis=0)

        def produce(d):
            w[d] = product(high, both, bhi[d, 0:cells], blo[d, 0:cells], ALONG)

        reduce_scatter(produce, w, ra, rt, pb)
        xg[j, mine] = jnp.zeros((BLOCK, 2 * LANES), F32)

        def consume(d):
            phigh, plow = split(pb[d])
            bhi[d, cells + SLOTS : cells + SLOTS + BLOCK] = phigh
            blo[d, cells + SLOTS : cells + SLOTS + BLOCK] = plow
            pboth = jnp.concatenate([phigh, plow], axis=0)
            xg[j, mine] = xg[j, mine] + product(phigh, pboth, bhi[d], blo[d], ROWS)

        all_gather(w, ra, rt, pb, consume)
        box = xg.at[j]
        spread(along_genes, box, mine, g, xs_sem.at[j], xr_sem.at[j])
        total = gathered(along_genes, box, mine, g, xs_sem.at[j], xr_sem.at[j])
        projected, factor, against, change = orthonormal(
            total[:, cells:], er[...], tr[...], mr[...], total[:, :cells]
        )
        couple_out[j] = factor
        later = pl.multiple_of(position + BLOCK, BLOCK)
        mr[pl.ds(later, BLOCK)] = projected
        er[pl.ds(later, BLOCK)] = er[pl.ds(later, BLOCK)] + against
        tr[pl.ds(later, BLOCK)] = against
        chigh, clow = split(change)
        cboth = jnp.concatenate([chigh, clow], axis=0)

        def right(d):
            fresh = product(chigh, cboth, bhi[d, cells:], blo[d, cells:], ALONG)
            vhigh, vlow = split(fresh)
            bhi[d, pl.ds(cells + later, BLOCK)] = vhigh
            blo[d, pl.ds(cells + later, BLOCK)] = vlow
            return fresh * scales[1]

        rows = pl.ds(position - BASIS, BLOCK)

        def emit(d):
            right_out[rows, pl.ds(pl.multiple_of(d * width, LANES), width)] = right(d)

        loop(0, whole, emit)
        if genes % width:
            right_out[rows, whole * width : genes] = right(whole)[:, : genes % width]

    loop(0, STEPS, step)


def body(counts, live_rows, left_basis, right_basis, right_start):
    cells, genes = counts.shape
    n = lax.axis_size("cells")
    g = lax.axis_size("genes")
    h = n // 2
    width = -(-(genes // LANES + 1) // n) * LANES
    scales = (math.sqrt(float(cells * n)), math.sqrt(float(genes * g)))
    vmem = pl.BlockSpec(memory_space=pltpu.VMEM)
    anywhere = pl.BlockSpec(memory_space=pl.ANY)
    square = pltpu.VMEM((LANES, LANES), F32)
    dma = lambda *shape: pltpu.SemaphoreType.DMA(shape)
    out_shape = (
        jax.ShapeDtypeStruct((STEPS * BLOCK, cells), F32),
        jax.ShapeDtypeStruct((STEPS * BLOCK, genes), F32),
        jax.ShapeDtypeStruct((STEPS, BLOCK, BLOCK), F32),
        jax.ShapeDtypeStruct((STEPS, BLOCK, BLOCK), F32),
    )
    buffers = lambda rows: [
        pltpu.VMEM((n, rows, width), F32),
        pltpu.VMEM((h, rows, width), F32),
        pltpu.VMEM((h, rows, width), F32),
        pltpu.VMEM((n, rows, width), F32),
    ]
    scratch = [
        pltpu.VMEM((n, cells, width), jnp.int32),
        pltpu.VMEM((n, cells, width), F32),
        pltpu.VMEM((n, cells + LANES, width), BF16),
        pltpu.VMEM((n, cells + LANES, width), BF16),
        pltpu.VMEM((n, BASIS + BLOCK, width), F32),
        square, square, square, square, square, square,
        *buffers(BLOCK),
        *buffers(8),
        pltpu.VMEM((n, BASIS, LANES), F32),
        pltpu.VMEM((n, BLOCK, LANES), F32),
        pltpu.VMEM((g, BASIS + BLOCK, 2 * LANES), F32),
        pltpu.VMEM((STEPS, g, BLOCK, 2 * LANES), F32),
        dma(n, 3),
        dma(h), dma(h), dma(h), dma(h), dma(h), dma(n), dma(h),
        dma(n), dma(n), dma(n), dma(n),
        dma(g), dma(g), dma(STEPS, g), dma(STEPS, g),
    ]
    return pl.pallas_call(
        functools.partial(kernel, n, g, width, scales),
        out_shape=out_shape,
        in_specs=[pl.BlockSpec(memory_space=pltpu.SMEM), anywhere, vmem, anywhere, anywhere],
        out_specs=(vmem, vmem, vmem, vmem),
        scratch_shapes=scratch,
        compiler_params=pltpu.CompilerParams(
            collective_id=0, has_side_effects=True, vmem_limit_bytes=66 * 1000 * 1000
        ),
    )(live_rows, counts, left_basis, right_basis, right_start)


def solution(mesh):
    in_specs = (
        P("cells", "genes"),
        P("cells"),
        P(None, "cells"),
        P(None, "genes"),
        P(None, "genes"),
    )
    out_specs = (P(None, "cells"), P(None, "genes"), P(), P())
    return jax.shard_map(body, mesh=mesh, in_specs=in_specs, out_specs=out_specs, check_vma=False)
```

time: 758 us -> 208 us (0.27)
  waiting for transfers between devices: 307 us -> 0 us
  blocking collectives: 250 us -> 0 us
  Pallas kernels: 0 us -> 197 us
  matrix products: 128 us -> 0 us
  other arithmetic: 42.6 us -> 0 us
  between operations: 15.9 us -> 1.29 us
    psum x4 -> x0, waiting for transfers between devices: 307 us -> none  [the longest x3 263 us: body(): lax.psum(projected, 'cells')]
    psum x10 -> x0, blocking collectives: 250 us -> none  [the longest x3 175 us: left_totals(): return lax.psum(values, 'cells')]
    pallas_call x0 -> x1, Pallas kernels: none -> 197 us  [body(): pl.pallas_call(functools.partial(kernel, n, g, width, scales), out_shape=...]
    dot_general x53 -> x0, matrix products: 119 us -> none  [the longest x29 69.6 us: outer_rows(): lax.dot_general(lhs, rhs, (((1,), (1,)), ((), ())), precision=HIGHEST, pr...]
    another operation x36 -> x0, other arithmetic: 28.1 us -> none  [the longest x18 12.8 us: orthonormal_block(): factor = jnp.linalg.cholesky(squares)]
    another operation x18 -> x0, matrix products: 8.49 us -> none  [lower_solve(): lax.linalg.triangular_solve(factor, values, left_side=True, lower=True)]
    reduce_sum x1 -> x0, other arithmetic: 7.68 us -> none  [body(): jnp.sum(logged, axis=0)]
  transfers between devices with their start and end apart: 4 -> 0, of which waited for: 4 -> 0; matrix products, arithmetic and copies ran while one was open for 2% -> 0% of each run, Pallas kernels for 0% -> 0%
where the time goes in v1:
time: 208 us; the launch traced here: 205 us
  Pallas kernels  197 us (95%)
  local copies, waits for them, and re-layouts  6.37 us (3%)
    pallas_call x1, Pallas kernels, body(): pl.pallas_call(functools.partial(kernel, n, g, width, scales), out_shape=...  197 us
    unnamed x8, local copies, waits for them, and re-layouts  6.37 us

profile of v1, /device:TPU:0, one launch (start us, length us, event | category | flops | bytes accessed | tf_op | source)
XLA Modules:
  0.0 204.6 jit_solution(3423875396658257011)
XLA Ops:
  1.3 197.0 %shard_map.84 = (f32[48,128]{1,0:T(8,128)}, f32[48,16640]{1,0:T(8,128)}, f32[3,16,16]{2,1,0:T(8,128)}, f32[3,16,16]{2,1,0:T(8,128)}) custom-call(s32[1]{0:T(128)S(6)} %copy.13.live, s32[128,16640]{1,0:T(8,128)} %counts.1, f32[32,128]{1,0:T(8,128)} %left_basis.1, f32[32,16640]{1,0:T(8,128)} %right_basis.1, f32[16,16640]{1,0:T(8,128)} %right_start.1), custom_call_target="tpu_custom_call" | custom-call | tf_op jit(solution)/shard_map/pallas_call | solution.py:422
  198.3 1.3 copy.14
  199.6 0.0 copy-start.1
  199.6 0.0 copy-start
  199.6 3.8 %copy.15 = f32[48,16640]{1,0:T(8,128)} copy(f32[48,16640]{1,0:T(8,128)} %get-tuple-element.9) | data formatting | bytes 6389760
  203.4 0.0 copy-done.1
  203.4 0.6 copy.16
  204.0 0.0 copy-done
  204.0 0.6 copy.17
Async XLA Ops:
  199.6 3.8 %copy-start.1 = (f32[3,16,16]{2,1,0:T(8,128)S(1)}, f32[3,16,16]{2,1,0:T(8,128)}, u32[]{:S(2)}) copy-start(f32[3,16,16]{2,1,0:T(8,128)} %get-tuple-element.10) | copy-start | bytes 9220
  199.6 4.4 %copy-start = (f32[3,16,16]{2,1,0:T(8,128)S(1)}, f32[3,16,16]{2,1,0:T(8,128)}, u32[]{:S(2)}) copy-start(f32[3,16,16]{2,1,0:T(8,128)} %get-tuple-element.11) | copy-start | bytes 9220

commit v2 on v1

--- a/solution.py
+++ b/solution.py
@@ -89,8 +89,8 @@
     live, counts, left_basis, right_basis, right_start,
     left_out, right_out, diag_out, couple_out,
     cnt, logged, bhi, blo, rb, sl, mr, el, tl, er, tr,
-    w, ra, rt, pb, w8, ra8, rt8, pb8, gram0, gram, xg0, xg,
-    in_sem, as_sem, ar_sem, bs_sem, br_sem, cs_sem, cr_sem, ds_sem,
+    w, ra, rt, rz, pb, w8, ra8, rt8, rz8, pb8, chg, gram0, gram, xg0, xg,
+    in_sem, as_sem, ar_sem, bs_sem, br_sem, cs_sem, cr_sem, ds_sem, fs_sem, zs_sem, zr_sem,
     g0s_sem, g0r_sem, gs_sem, gr_sem, x0s_sem, x0r_sem, xs_sem, xr_sem,
 ):
     cells, genes = counts.shape
@@ -99,6 +99,10 @@
     core = lax.rem(me, 2)
     chip = me // 2
     h = n // 2
+    b = 1 << ((h.bit_length() - 1) // 2)
+    b = b if h % b == 0 else 1
+    a = h // b
+    zi, yi = chip // b, lax.rem(chip, b)
     sibling = me + 1 - 2 * core
 
     def along_cells(src, dst, send, recv, peer):
@@ -162,9 +166,13 @@
             1, size, lambda k, total: total + buf[k], buf[0]
         )
 
-    def reduce_scatter(produce, part, fromcore, fromchips, result):
+    def order(k):
+        return lax.rem(zi + 1 + lax.rem(k, a), a), lax.rem(yi + 1 + k // a, b)
+
+    def reduce_scatter(produce, part, fromcore, fromy, fromz, result):
         def first(k):
-            t = lax.rem(chip + 1 + k, h)
+            z, y = order(k)
+            t = z * b + y
             d = 2 * t + 1 - core
             produce(d)
             along_cells(part.at[d], fromcore.at[t], as_sem.at[t], ar_sem.at[t], sibling).start()
@@ -179,43 +187,88 @@
             return d
 
         def second(k):
-            t = lax.rem(chip + 1 + k, h)
+            z, y = order(k)
+            t = z * b + y
             d = join(t)
-            along_cells(part.at[d], fromchips.at[chip], bs_sem.at[t], br_sem.at[chip], d).start()
-
-        loop(0, h - 1, second)
-        join(chip)
+            to = z * b + yi
+            along_cells(part.at[d], fromy.at[to], bs_sem.at[t], br_sem.at[to], 2 * (zi * b + y) + core).start()
+
+        loop(0, h - a, second)
+
+        def complete(z):
+            d = join(z * b + yi)
+
+            def add(k):
+                source = z * b + lax.rem(yi + k, b)
+                along_cells(part.at[d], fromy.at[source], bs_sem.at[source], br_sem.at[source], sibling).wait_recv()
+                part[d] = part[d] + fromy[source]
+
+            loop(1, b, add)
+            return d
+
+        def third(k):
+            z = lax.rem(zi + k, a)
+            d = complete(z)
+            along_cells(part.at[d], fromz.at[zi], zs_sem.at[z], zr_sem.at[zi], d).start()
+
+        loop(1, a, third)
+        complete(zi)
         result[me] = part[me]
 
-        def third(k):
-            t = lax.rem(chip + h - k, h)
-            along_cells(part.at[me], fromchips.at[t], bs_sem.at[t], br_sem.at[t], sibling).wait_recv()
-            result[me] = result[me] + fromchips[t]
-
-        loop(1, h, third)
-
-    def all_gather(part, fromcore, fromchips, result, consume):
+        def fourth(k):
+            z = lax.rem(zi + a - k, a)
+            along_cells(part.at[me], fromz.at[z], zs_sem.at[z], zr_sem.at[z], sibling).wait_recv()
+            result[me] = result[me] + fromz[z]
+
+        loop(1, a, fourth)
+
+    def all_gather(part, fromcore, fromy, fromz, result, consume):
+        def relay(z):
+            t = z * b + yi
+            d = 2 * t + core
+
+            def to_y(k):
+                y = lax.rem(yi + k, b)
+                along_cells(result.at[d], result.at[d], fs_sem.at[z * b + y], cr_sem.at[d], 2 * (zi * b + y) + core).start()
+
+            loop(1, b, to_y)
+            along_cells(result.at[d], result.at[d], ds_sem.at[t], cr_sem.at[d], sibling).start()
+
+        def arrived(d):
+            along_cells(result.at[d], result.at[d], ds_sem.at[0], cr_sem.at[d], sibling).wait_recv()
+
         def go(k):
-            t = lax.rem(chip + k, h)
-            along_cells(result.at[me], result.at[me], cs_sem.at[t], cr_sem.at[me], 2 * t + core).start()
-
-        loop(1, h, go)
-        along_cells(result.at[me], result.at[me], ds_sem.at[chip], cr_sem.at[me], sibling).start()
+            z = lax.rem(zi + k, a)
+            along_cells(result.at[me], result.at[me], cs_sem.at[z], cr_sem.at[me], 2 * (z * b + yi) + core).start()
+
+        loop(1, a, go)
+        relay(zi)
         consume(me)
 
-        def pass_on(k):
-            t = lax.rem(chip + h - k, h)
+        def pass_z(k):
+            z = lax.rem(zi + a - k, a)
+            d = 2 * (z * b + yi) + core
+            arrived(d)
+            relay(z)
+            consume(d)
+
+        loop(1, a, pass_z)
+
+        def pass_y(k):
+            z = lax.rem(zi + a - lax.rem(k, a), a)
+            t = z * b + lax.rem(yi + 1 + k // a, b)
             d = 2 * t + core
-            along_cells(result.at[d], result.at[d], cs_sem.at[t], cr_sem.at[d], sibling).wait_recv()
+            arrived(d)
             along_cells(result.at[d], result.at[d], ds_sem.at[t], cr_sem.at[d], sibling).start()
             consume(d)
 
-        loop(1, h, pass_on)
+        loop(0, h - a, pass_y)
 
         def rest(k):
-            t = lax.rem(chip + h - k, h)
+            z = lax.rem(zi + a - lax.rem(k, a), a)
+            t = z * b + lax.rem(yi + k // a, b)
             d = 2 * t + 1 - core
-            along_cells(result.at[d], result.at[d], cs_sem.at[t], cr_sem.at[d], sibling).wait_recv()
+            arrived(d)
             consume(d)
 
         loop(0, h, rest)
@@ -226,12 +279,20 @@
 
         loop(0, h, ended)
 
-        def ended_chips(k):
-            t = lax.rem(chip + k, h)
-            along_cells(part.at[t], fromchips.at[t], bs_sem.at[t], br_sem.at[t], sibling).wait_send()
-            along_cells(result.at[t], result.at[t], cs_sem.at[t], cr_sem.at[t], sibling).wait_send()
-
-        loop(1, h, ended_chips)
+        def ended_y(k):
+            z, y = order(k)
+            t = z * b + y
+            along_cells(part.at[t], fromy.at[t], bs_sem.at[t], br_sem.at[t], sibling).wait_send()
+            along_cells(result.at[t], result.at[t], fs_sem.at[t], cr_sem.at[t], sibling).wait_send()
+
+        loop(0, h - a, ended_y)
+
+        def ended_z(k):
+            z = lax.rem(zi + k, a)
+            along_cells(part.at[z], fromz.at[z], zs_sem.at[z], zr_sem.at[z], sibling).wait_send()
+            along_cells(result.at[z], result.at[z], cs_sem.at[z], cr_sem.at[z], sibling).wait_send()
+
+        loop(1, a, ended_z)
 
     live_here = live[0]
     weights_row = jnp.where(
@@ -270,7 +331,7 @@
         lax.broadcasted_iota(jnp.int32, (8, LANES), 0) == 0, live_here.astype(F32), 0.0
     )
 
-    reduce_scatter(lambda d: None, w8, ra8, rt8, pb8)
+    reduce_scatter(lambda d: None, w8, ra8, rt8, rz8, pb8)
     for _, trio in loads:
         trio[1].wait()
         trio[2].wait()
@@ -284,7 +345,7 @@
         blo[d, cells + BASIS + BLOCK :] = blank
 
     loop(0, n, fill)
-    all_gather(w8, ra8, rt8, pb8, lambda d: None)
+    all_gather(w8, ra8, rt8, rz8, pb8, lambda d: None)
     live_total = jnp.sum(
         pb8[total_at, :, total_lane : total_lane + LANES], axis=0, keepdims=True
     )
@@ -315,12 +376,35 @@
     er[0 : BASIS + BLOCK] = cross[:, cells:]
     whole = genes // width
 
+    def update(j):
+        later = cells + BASIS + (j + 1) * BLOCK
+        later = later if isinstance(j, int) else pl.multiple_of(later, BLOCK)
+        chigh, clow = split(chg[...])
+        cboth = jnp.concatenate([chigh, clow], axis=0)
+
+        def right(d):
+            fresh = product(chigh, cboth, bhi[d, cells:], blo[d, cells:], ALONG)
+            vhigh, vlow = split(fresh)
+            bhi[d, pl.ds(later, BLOCK)] = vhigh
+            blo[d, pl.ds(later, BLOCK)] = vlow
+            return fresh * scales[1]
+
+        rows = pl.ds(j * BLOCK if isinstance(j, int) else pl.multiple_of(j * BLOCK, BLOCK), BLOCK)
+
+        def emit(d):
+            right_out[rows, pl.ds(pl.multiple_of(d * width, LANES), width)] = right(d)
+
+        loop(0, whole, emit)
+        if genes % width:
+            right_out[rows, whole * width : genes] = right(whole)[:, : genes % width]
+
     def step(j):
         position = pl.multiple_of(BASIS + j * BLOCK, BLOCK)
         vectors = mr[pl.ds(position, BLOCK)]
         sl[SLOTS : SLOTS + BLOCK] = vectors
         gram[me] = exact_rows(vectors, sl[...])
         spread(along_cells, gram, me, n, gs_sem, gr_sem)
+        pl.when(j > 0)(lambda: update(j - 1))
         total = gathered(along_cells, gram, me, n, gs_sem, gr_sem)
         leftvec, factor, against, _ = orthonormal(total, el[...], tl[...], sl[...], vectors)
         diag_out[j] = factor
@@ -334,7 +418,7 @@
         def produce(d):
             w[d] = product(high, both, bhi[d, 0:cells], blo[d, 0:cells], ALONG)
 
-        reduce_scatter(produce, w, ra, rt, pb)
+        reduce_scatter(produce, w, ra, rt, rz, pb)
         xg[j, mine] = jnp.zeros((BLOCK, 2 * LANES), F32)
 
         def consume(d):
@@ -344,7 +428,7 @@
             pboth = jnp.concatenate([phigh, plow], axis=0)
             xg[j, mine] = xg[j, mine] + product(phigh, pboth, bhi[d], blo[d], ROWS)
 
-        all_gather(w, ra, rt, pb, consume)
+        all_gather(w, ra, rt, rz, pb, consume)
         box = xg.at[j]
         spread(along_genes, box, mine, g, xs_sem.at[j], xr_sem.at[j])
         total = gathered(along_genes, box, mine, g, xs_sem.at[j], xr_sem.at[j])
@@ -356,26 +440,10 @@
         mr[pl.ds(later, BLOCK)] = projected
         er[pl.ds(later, BLOCK)] = er[pl.ds(later, BLOCK)] + against
         tr[pl.ds(later, BLOCK)] = against
-        chigh, clow = split(change)
-        cboth = jnp.concatenate([chigh, clow], axis=0)
-
-        def right(d):
-            fresh = product(chigh, cboth, bhi[d, cells:], blo[d, cells:], ALONG)
-            vhigh, vlow = split(fresh)
-            bhi[d, pl.ds(cells + later, BLOCK)] = vhigh
-            blo[d, pl.ds(cells + later, BLOCK)] = vlow
-            return fresh * scales[1]
-
-        rows = pl.ds(position - BASIS, BLOCK)
-
-        def emit(d):
-            right_out[rows, pl.ds(pl.multiple_of(d * width, LANES), width)] = right(d)
-
-        loop(0, whole, emit)
-        if genes % width:
-            right_out[rows, whole * width : genes] = right(whole)[:, : genes % width]
+        chg[...] = change
 
     loop(0, STEPS, step)
+    update(STEPS - 1)
 
 
 def body(counts, live_rows, left_basis, right_basis, right_start):
@@ -399,6 +467,7 @@
         pltpu.VMEM((n, rows, width), F32),
         pltpu.VMEM((h, rows, width), F32),
         pltpu.VMEM((h, rows, width), F32),
+        pltpu.VMEM((h, rows, width), F32),
         pltpu.VMEM((n, rows, width), F32),
     ]
     scratch = [
@@ -410,12 +479,13 @@
         square, square, square, square, square, square,
         *buffers(BLOCK),
         *buffers(8),
+        pltpu.VMEM((BLOCK, LANES), F32),
         pltpu.VMEM((n, BASIS, LANES), F32),
         pltpu.VMEM((n, BLOCK, LANES), F32),
         pltpu.VMEM((g, BASIS + BLOCK, 2 * LANES), F32),
         pltpu.VMEM((STEPS, g, BLOCK, 2 * LANES), F32),
         dma(n, 3),
-        dma(h), dma(h), dma(h), dma(h), dma(h), dma(n), dma(h),
+        dma(h), dma(h), dma(h), dma(h), dma(h), dma(n), dma(h), dma(h), dma(h), dma(h),
         dma(n), dma(n), dma(n), dma(n),
         dma(g), dma(g), dma(STEPS, g), dma(STEPS, g),
     ]

time: 208 us -> 181 us (0.87); the launches traced: 205 us -> 181 us
  Pallas kernels: 197 us -> 173 us
    pallas_call x1, Pallas kernels: 197 us -> 173 us  [body(): pl.pallas_call(functools.partial(kernel, n, g, width, scales), out_shape=...]
where the time goes in v2:
time: 181 us
  Pallas kernels  173 us (96%)
  local copies, waits for them, and re-layouts  6.37 us (4%)
    pallas_call x1, Pallas kernels, body(): pl.pallas_call(functools.partial(kernel, n, g, width, scales), out_shape=...  173 us
    unnamed x8, local copies, waits for them, and re-layouts  6.37 us

profile of v2, /device:TPU:0, one launch (start us, length us, event | category | flops | bytes accessed | tf_op | source)
XLA Modules:
  0.0 181.0 jit_solution(15812471712394309359)
XLA Ops:
  1.3 173.3 %shard_map.84 = (f32[48,128]{1,0:T(8,128)}, f32[48,16640]{1,0:T(8,128)}, f32[3,16,16]{2,1,0:T(8,128)}, f32[3,16,16]{2,1,0:T(8,128)}) custom-call(s32[1]{0:T(128)S(6)} %copy.13.live, s32[128,16640]{1,0:T(8,128)} %counts.1, f32[32,128]{1,0:T(8,128)} %left_basis.1, f32[32,16640]{1,0:T(8,128)} %right_basis.1, f32[16,16640]{1,0:T(8,128)} %right_start.1), custom_call_target="tpu_custom_call" | custom-call | tf_op jit(solution)/shard_map/pallas_call | solution.py:492
  174.6 1.3 copy.14
  176.0 0.0 copy-start.1
  176.0 0.0 copy-start
  176.0 3.8 %copy.15 = f32[48,16640]{1,0:T(8,128)} copy(f32[48,16640]{1,0:T(8,128)} %get-tuple-element.9) | data formatting | bytes 6389760
  179.8 0.0 copy-done.1
  179.8 0.6 copy.16
  180.4 0.0 copy-done
  180.4 0.6 copy.17
Async XLA Ops:
  176.0 3.8 %copy-start.1 = (f32[3,16,16]{2,1,0:T(8,128)S(1)}, f32[3,16,16]{2,1,0:T(8,128)}, u32[]{:S(2)}) copy-start(f32[3,16,16]{2,1,0:T(8,128)} %get-tuple-element.10) | copy-start | bytes 9220
  176.0 4.4 %copy-start = (f32[3,16,16]{2,1,0:T(8,128)S(1)}, f32[3,16,16]{2,1,0:T(8,128)}, u32[]{:S(2)}) copy-start(f32[3,16,16]{2,1,0:T(8,128)} %get-tuple-element.11) | copy-start | bytes 9220

commit v3 on v2

--- a/solution.py
+++ b/solution.py
@@ -250,9 +250,9 @@
             d = 2 * (z * b + yi) + core
             arrived(d)
             relay(z)
-            consume(d)
 
         loop(1, a, pass_z)
+        loop(1, a, lambda k: consume(2 * (lax.rem(zi + a - k, a) * b + yi) + core))
 
         def pass_y(k):
             z = lax.rem(zi + a - lax.rem(k, a), a)

time: 181 us -> 181 us (level)
  no operation moved by 1% of the time
where the time goes in v3:
time: 181 us
  Pallas kernels  173 us (96%)
  local copies, waits for them, and re-layouts  6.37 us (4%)
    pallas_call x1, Pallas kernels, body(): pl.pallas_call(functools.partial(kernel, n, g, width, scales), out_shape=...  173 us
    unnamed x8, local copies, waits for them, and re-layouts  6.37 us

profile of v3, /device:TPU:0, one launch (start us, length us, event | category | flops | bytes accessed | tf_op | source)
XLA Modules:
  0.0 181.0 jit_solution(15896511785507735447)
XLA Ops:
  1.3 173.3 %shard_map.84 = (f32[48,128]{1,0:T(8,128)}, f32[48,16640]{1,0:T(8,128)}, f32[3,16,16]{2,1,0:T(8,128)}, f32[3,16,16]{2,1,0:T(8,128)}) custom-call(s32[1]{0:T(128)S(6)} %copy.13.live, s32[128,16640]{1,0:T(8,128)} %counts.1, f32[32,128]{1,0:T(8,128)} %left_basis.1, f32[32,16640]{1,0:T(8,128)} %right_basis.1, f32[16,16640]{1,0:T(8,128)} %right_start.1), custom_call_target="tpu_custom_call" | custom-call | tf_op jit(solution)/shard_map/pallas_call | solution.py:492
  174.6 1.3 copy.14
  176.0 0.0 copy-start.1
  176.0 0.0 copy-start
  176.0 3.8 %copy.15 = f32[48,16640]{1,0:T(8,128)} copy(f32[48,16640]{1,0:T(8,128)} %get-tuple-element.9) | data formatting | bytes 6389760
  179.8 0.0 copy-done.1
  179.8 0.6 copy.16
  180.4 0.0 copy-done
  180.4 0.6 copy.17
Async XLA Ops:
  176.0 3.8 %copy-start.1 = (f32[3,16,16]{2,1,0:T(8,128)S(1)}, f32[3,16,16]{2,1,0:T(8,128)}, u32[]{:S(2)}) copy-start(f32[3,16,16]{2,1,0:T(8,128)} %get-tuple-element.10) | copy-start | bytes 9220
  176.0 4.4 %copy-start = (f32[3,16,16]{2,1,0:T(8,128)S(1)}, f32[3,16,16]{2,1,0:T(8,128)}, u32[]{:S(2)}) copy-start(f32[3,16,16]{2,1,0:T(8,128)} %get-tuple-element.11) | copy-start | bytes 9220
